TPU v7x, 128 devices: a whole 4x4x4 slice. The times are simulated.
128 devices in a mesh: tp: 8 (over y, x_hi), dp: 16 (over z, x_lo, core).
Axes of the slice: x: 4 (x_hi: 2, x_lo: 2; x = x_hi * 2 + x_lo), y: 4, z: 4, core: 2. Of those that a mesh axis runs over, the one named last changes fastest.
Arguments:
- activations: bfloat16 [2, 16384, 8192], P(None, 'dp', 'tp'), may hold values from -72 to 72
- out_grads: bfloat16 [2, 16384, 2048], P(None, 'dp'), may hold values from -2 to 2
- master: float32 [8192, 2, 2048], P(('tp', 'dp')), may hold values from -1.2 to 1.2
- first_moment: float32 [8192, 2, 2048], P(('tp', 'dp')), may hold values from -1.8 to 1.8
- second_moment: float32 [8192, 2, 2048], P(('tp', 'dp')), may hold values from 0.01 to 1
Outputs:
- new_master: float32 [8192, 2, 2048], P(('tp', 'dp'))
- new_first: float32 [8192, 2, 2048], P(('tp', 'dp'))
- new_second: float32 [8192, 2, 2048], P(('tp', 'dp'))
- weights: bfloat16 [8192, 2, 2048], P('tp')
All inputs are finite; a program needn't handle non-finite values.
Results may differ from a plain program's by a relative error of at most 0.0004.
Values may be sent and summed in bfloat16 or wider, within the bound.
A program may use at most 128 MiB of HBM per device.

v0:
```python
import functools
import math
import jax
import jax.numpy as jnp
from jax import lax
from jax.sharding import Mesh
from jax.sharding import PartitionSpec as P

DP = ("dp_0", "dp_1", "dp_2")
TP_DP = ("tp_0", "tp_1", "dp_0", "dp_1", "dp_2")
TP = ("tp_0", "tp_1")
beta_first = 0.9
beta_second = 0.95
first_fix = 1.0 - 0.9**10
second_fix = 1.0 - 0.95**10
learn_rate = 0.01
decay_rate = 0.1
epsilon = 1e-08
limit_scale = 2.0


def cut_along(array, dim, peers):
    dims = array.shape
    blocks = array.reshape(*dims[:dim], peers, dims[dim] // peers, *dims[dim + 1 :])
    return jnp.moveaxis(blocks, dim, 0)


def scatter_pairs(array, chips, core, dim):
    sizes = (lax.axis_size(chips), lax.axis_size(core))
    blocks = cut_along(array, dim, sizes[0] * sizes[1])
    inside = blocks.shape[1:]
    blocks = blocks.reshape(*sizes, *inside).swapaxes(0, 1).reshape(-1, *inside)
    blocks = lax.psum_scatter(blocks, core, scatter_dimension=0, tiled=True)
    return lax.psum_scatter(blocks, chips, scatter_dimension=0, tiled=True)[0]


def one_axis_at_a_time(array, axes):
    return functools.reduce(lax.psum, axes, array)


def reduce_rows(layer_acts, layer_grads):
    grad_own = scatter_pairs(
        jnp.einsum("ltr,ltc->rlc", layer_acts, layer_grads, preferred_element_type=jnp.float32),
        ("dp_0", "dp_1"),
        "dp_2",
        0,
    )
    partial_value = jnp.sum(grad_own * grad_own)
    return (grad_own, partial_value)


def adam_update(grad_own, master, first_moment, second_moment, clip_factor):
    clipped = clip_factor * grad_own
    new_first = beta_first * first_moment + (1.0 - beta_first) * clipped
    new_second = beta_second * second_moment + (1.0 - beta_second) * clipped * clipped
    step_dir = new_first / first_fix / (jnp.sqrt(new_second / second_fix) + epsilon)
    new_master = master - learn_rate * (step_dir + decay_rate * master)
    return (new_master, new_first, new_second)


def on_device(activations, out_grads, master, first_moment, second_moment):
    own_rows = master.shape[0]
    grad_own, layer_sum = reduce_rows(activations, out_grads)
    sum_squares = one_axis_at_a_time(layer_sum, TP_DP)
    entries = own_rows * lax.axis_size(TP) * lax.axis_size(DP) * master.shape[1] * master.shape[2]
    limit = limit_scale * math.sqrt(entries)
    clip_factor = limit / jnp.maximum(jnp.sqrt(sum_squares), limit)
    new_master, new_first, new_second = adam_update(
        grad_own, master, first_moment, second_moment, clip_factor
    )
    rounded = new_master.astype(jnp.bfloat16)
    tp_rows = lax.all_gather(rounded, DP, axis=0, tiled=True)
    return (new_master, new_first, new_second, tp_rows)


def solution(mesh):
    finer = Mesh(mesh.devices.reshape(4, 2, 4, 2, 2), ("tp_0", "tp_1", "dp_0", "dp_1", "dp_2"))
    in_specs = (
        P(None, DP, TP),
        P(None, DP, None),
        P(TP_DP, None, None),
        P(TP_DP, None, None),
        P(TP_DP, None, None),
    )
    out_specs = (
        P(TP_DP, None, None),
        P(TP_DP, None, None),
        P(TP_DP, None, None),
        P(TP, None, None),
    )
    return jax.shard_map(
        on_device, mesh=finer, in_specs=in_specs, out_specs=out_specs, check_vma=False
    )
```

profile of v0, /device:TPU:1, one launch (start us, length us, event | category | flops | bytes accessed | tf_op | source)
XLA Modules:
  0.0 349.5 jit_solution(12573614637732273600)
XLA Ops:
  7.2 0.0 reduce-scatter.3.cloned.1.call-start
  7.2 15.8 %fusion.5 = f32[2,2048,1024]{1,2,0:T(8,128)} fusion(bf16[2,1024,2048]{2,1,0:T(8,128)(2,1)} %param.6, bf16[2,1024,1024]{2,1,0:T(8,128)(2,1)} %param.5), kind=kOutput, calls=%fused_computation.9 | convolution fusion | flops 8589934592 | bytes 29360128 | tf_op jit(solution)/shard_map/ltr,ltc->rlc/dot_general | solution.py:43
  23.0 11.6 %copy.13 = f32[2,8,64,2,2048]{4,2,3,1,0:T(8,128)} copy(f32[2,8,64,2,2048]{4,2,0,1,3:T(8,128)} %bitcast.16) | data formatting | bytes 33554432 | tf_op jit(solution)/shard_map/transpose | solution.py:32
  34.7 0.0 reduce-scatter.3.cloned.1.call-update
  34.7 0.0 reduce-scatter.5.cloned.1.call-start
  34.7 31.5 %reduce-scatter.3.cloned.1.call-done = f32[8,64,2,2048]{3,1,2,0:T(8,128)} async-done(((f32[16,64,2,2048]{3,1,2,0:T(8,128)}), f32[8,64,2,2048]{3,1,2,0:T(8,128)}) %reduce-scatter.3.cloned.1.call-update) | async-done | bytes 8388624 | tf_op jit(solution)/shard_map/reduce_scatter | solution.py:33
  66.2 0.0 reduce-scatter.5.cloned.1.call-update
  66.2 0.0 all-gather.2.cloned.1.call-start
  66.3 172.5 %reduce-scatter.5.cloned.1.call-done = f32[1,64,2,2048]{3,1,2,0:T(8,128)} async-done(((f32[8,64,2,2048]{3,1,2,0:T(8,128)}), f32[1,64,2,2048]{3,1,2,0:T(8,128)}) %reduce-scatter.5.cloned.1.call-update) | async-done | bytes 1048592 | tf_op jit(solution)/shard_map/reduce_scatter | solution.py:34
  238.8 2.1 multiply_reduce_fusion
  240.9 9.1 %psum.35 = f32[]{:T(128)} all-reduce(f32[]{:T(128)} %multiply_reduce_fusion), channel_id=1, replica_groups=mesh['tp_0'=4,'tp_1'=2,'dp_0'=4,'dp_1'=2,'dp_2'=2] {'tp_0'}, use_global_device_ids=true, to_apply=%region_3.0 | all-reduce | flops 1 | bytes 8 | tf_op jit(solution)/shard_map/psum | solution.py:38
  250.0 5.9 %psum.36 = f32[]{:T(128)} all-reduce(f32[]{:T(128)} %psum.35), channel_id=1, replica_groups=mesh['tp_0'=4,'tp_1'=2,'dp_0'=4,'dp_1'=2,'dp_2'=2] {'tp_1'}, use_global_device_ids=true, to_apply=%region_4.0 | all-reduce | flops 1 | bytes 8 | tf_op jit(solution)/shard_map/psum | solution.py:38
  255.8 9.3 %psum.37 = f32[]{:T(128)} all-reduce(f32[]{:T(128)} %psum.36), channel_id=1, replica_groups=mesh['tp_0'=4,'tp_1'=2,'dp_0'=4,'dp_1'=2,'dp_2'=2] {'dp_0'}, use_global_device_ids=true, to_apply=%region_5.0 | all-reduce | flops 1 | bytes 8 | tf_op jit(solution)/shard_map/psum | solution.py:38
  265.1 4.4 %psum.38 = f32[]{:T(128)} all-reduce(f32[]{:T(128)} %psum.37), channel_id=1, replica_groups=mesh['tp_0'=4,'tp_1'=2,'dp_0'=4,'dp_1'=2,'dp_2'=2] {'dp_1'}, use_global_device_ids=true, to_apply=%region_6.0 | all-reduce | flops 1 | bytes 8 | tf_op jit(solution)/shard_map/psum | solution.py:38
  269.5 10.0 %psum.39 = f32[]{:T(128)} all-reduce(f32[]{:T(128)} %psum.38), channel_id=1, replica_groups=mesh['tp_0'=4,'tp_1'=2,'dp_0'=4,'dp_1'=2,'dp_2'=2] {'dp_2'}, use_global_device_ids=true, to_apply=%region_7.0 | all-reduce | flops 1 | bytes 8 | tf_op jit(solution)/shard_map/psum | solution.py:38
  280.3 4.5 %fusion.2 = (bf16[64,2,2048]{2,0,1:T(8,128)(2,1)S(1)}, f32[64,2,2048]{2,0,1:T(8,128)S(1)}, f32[64,2,2048]{2,0,1:T(8,128)S(1)}, f32[64,2,2048]{2,0,1:T(8,128)S(1)}) fusion(f32[64,2,2048]{2,1,0:T(2,128)} %param.7, f32[1,64,2,2048]{3,1,2,0:T(8,128)} %reduce-scatter.5.cloned.1.call-done, f32[]{:T(128)S(6)} %div.18, f32[64,2,2048]{2,1,0:T(2,128)} %param.8, ...), kind=kLoop, calls=%fused_computation.8 | loop fusion | flops 4456448 | bytes 7864324 | tf_op jit(solution)/shard_map/convert_element_type | solution.py:71
  284.8 1.3 copy.17
  286.1 0.0 all-gather.2.cloned.1.call-update
  286.1 1.8 copy.18
  287.9 1.8 copy.19
  289.7 1.8 copy.20
  291.5 43.5 %all-gather.2.cloned.1.call-done = bf16[1024,2,2048]{2,1,0:T(2,128)(2,1)} async-done(((bf16[64,2,2048]{2,1,0:T(2,128)(2,1)}), bf16[1024,2,2048]{2,1,0:T(2,128)(2,1)}) %all-gather.2.cloned.1.call-update) | async-done | bytes 8388624 | tf_op jit(solution)/shard_map/all_gather | solution.py:72
  335.0 8.0 %copy.33 = bf16[1024,2,2048]{2,1,0:T(2,128)(2,1)} copy(bf16[1024,2,2048]{2,1,0:T(2,128)(2,1)} %all-gather.2.cloned.1.call-done) | data formatting | bytes 16777216
Async XLA Ops:
  7.2 59.0 %reduce-scatter.3.cloned.1.call-start = ((), (), s32[]{:S(2)}) async-start(), calls=%async_computation.2 | async-start | bytes 25165824 | tf_op jit(solution)/shard_map/reduce_scatter | solution.py:33
  34.7 204.1 %reduce-scatter.5.cloned.1.call-start = ((), (), s32[]{:S(2)}) async-start(), calls=%async_computation.3 | async-start | bytes 9437184 | tf_op jit(solution)/shard_map/reduce_scatter | solution.py:34
  66.2 268.8 %all-gather.2.cloned.1.call-start = ((), (), s32[]{:S(2)}) async-start(), calls=%async_computation.4 | async-start | bytes 8912896 | tf_op jit(solution)/shard_map/all_gather | solution.py:72
Sparse Core Ops, SparseCore 0:
  34.8 31.3 reduce-scatter.2
  68.6 170.1 reduce-scatter.4
  286.2 48.6 all-gather.1
where the time goes:
time: 350 us; the launch traced here: 349 us
  waiting for transfers between devices  248 us (71%)
  blocking collectives  38.6 us (11%)
  local copies, waits for them, and re-layouts  26.3 us (8%)
  matrix products  15.8 us (5%)
  between operations  14.5 us (4%)
  other arithmetic  6.61 us (2%)
    reduce_scatter x1, waiting for transfers between devices, scatter_pairs(): return lax.psum_scatter(blocks, chips, scatter_dimension=0, tiled=True)[0]  173 us
    all_gather x1, waiting for transfers between devices, on_device(): tp_rows = lax.all_gather(rounded, DP, axis=0, tiled=True)  43.5 us
    psum x5, blocking collectives, one_axis_at_a_time(): return functools.reduce(lax.psum, axes, array)  38.6 us
    reduce_scatter x1, waiting for transfers between devices, scatter_pairs(): blocks = lax.psum_scatter(blocks, core, scatter_dimension=0, tiled=True)  31.5 us
    dot_general x1, matrix products, reduce_rows(): jnp.einsum('ltr,ltc->rlc', layer_acts, layer_grads, preferred_element_typ...  15.8 us
    unnamed x4, local copies, waits for them, and re-layouts  13.3 us
    transpose x1, local copies, waits for them, and re-layouts, scatter_pairs(): blocks = blocks.reshape(*sizes, *inside).swapaxes(0, 1).reshape(-1, *inside)  11.6 us
  transfers between devices with their start and end apart: 3, of which 3 were waited for; matrix products, arithmetic and copies ran while one was open for 2% of the time, Pallas kernels for 0%

commit v1 on v0

--- a/solution.py
+++ b/solution.py
@@ -69,7 +69,9 @@
         grad_own, master, first_moment, second_moment, clip_factor
     )
     rounded = new_master.astype(jnp.bfloat16)
-    tp_rows = lax.all_gather(rounded, DP, axis=0, tiled=True)
+    tp_rows = jnp.concatenate(
+        lax.all_to_all(jnp.stack([rounded] * lax.axis_size(DP)), DP, 0, 0), axis=0
+    )
     return (new_master, new_first, new_second, tp_rows)
 
 

time: 350 us -> 407 us (1.16)
  waiting for transfers between devices: 248 us -> 293 us
  local copies, waits for them, and re-layouts: 26.3 us -> 33.1 us
  starting transfers between devices: 0.12 us -> 4.92 us
    all_to_all x0 -> x1, waiting for transfers between devices: none -> 89.2 us  [on_device(): lax.all_to_all(jnp.stack([rounded] * lax.axis_size(DP)), DP, 0, 0)]
    all_gather x1 -> x0, waiting for transfers between devices: 43.5 us -> none  [on_device(): tp_rows = lax.all_gather(rounded, DP, axis=0, tiled=True)]
    another operation x0 -> x1, local copies, waits for them, and re-layouts: none -> 7.59 us  [on_device(): jnp.stack([rounded] * lax.axis_size(DP))]
    all_to_all x0 -> x1, starting transfers between devices: none -> 4.84 us  [on_device(): lax.all_to_all(jnp.stack([rounded] * lax.axis_size(DP)), DP, 0, 0)]
  transfers between devices with their start and end apart: 3 -> 3, of which waited for: 3 -> 3; matrix products, arithmetic and copies ran while one was open for 2% -> 1% of each run, Pallas kernels for 0% -> 0%
where the time goes in v1:
time: 407 us
  waiting for transfers between devices  293 us (72%)
  blocking collectives  38.4 us (9%)
  local copies, waits for them, and re-layouts  33.1 us (8%)
  matrix products  15.8 us (4%)
  between operations  14.8 us (4%)
  other arithmetic  6.61 us (2%)
  starting transfers between devices  4.92 us (1%)
    reduce_scatter x1, waiting for transfers between devices, scatter_pairs(): return lax.psum_scatter(blocks, chips, scatter_dimension=0, tiled=True)[0]  173 us
    all_to_all x1, waiting for transfers between devices, on_device(): lax.all_to_all(jnp.stack([rounded] * lax.axis_size(DP)), DP, 0, 0)  89.2 us
    psum x5, blocking collectives, one_axis_at_a_time(): return functools.reduce(lax.psum, axes, array)  38.4 us
    reduce_scatter x1, waiting for transfers between devices, scatter_pairs(): blocks = lax.psum_scatter(blocks, core, scatter_dimension=0, tiled=True)  31.5 us
    dot_general x1, matrix products, reduce_rows(): jnp.einsum('ltr,ltc->rlc', layer_acts, layer_grads, preferred_element_typ...  15.8 us
    unnamed x4, local copies, waits for them, and re-layouts  13.3 us
    transpose x1, local copies, waits for them, and re-layouts, scatter_pairs(): blocks = blocks.reshape(*sizes, *inside).swapaxes(0, 1).reshape(-1, *inside)  11.6 us
  transfers between devices with their start and end apart: 3, of which 3 were waited for; matrix products, arithmetic and copies ran while one was open for 1% of the time, Pallas kernels for 0%

profile of v1, /device:TPU:1, one launch (start us, length us, event | category | flops | bytes accessed | tf_op | source)
XLA Modules:
  0.0 406.9 jit_solution(1105197506466815787)
XLA Ops:
  7.2 0.0 reduce-scatter.3.cloned.1.call-start
  7.2 15.8 %fusion.5 = f32[2,2048,1024]{1,2,0:T(8,128)} fusion(bf16[2,1024,2048]{2,1,0:T(8,128)(2,1)} %param.6, bf16[2,1024,1024]{2,1,0:T(8,128)(2,1)} %param.5), kind=kOutput, calls=%fused_computation.9 | convolution fusion | flops 8589934592 | bytes 29360128 | tf_op jit(solution)/shard_map/ltr,ltc->rlc/dot_general | solution.py:43
  23.0 11.6 %copy.13 = f32[2,8,64,2,2048]{4,2,3,1,0:T(8,128)} copy(f32[2,8,64,2,2048]{4,2,0,1,3:T(8,128)} %bitcast.17) | data formatting | bytes 33554432 | tf_op jit(solution)/shard_map/transpose | solution.py:32
  34.7 0.0 reduce-scatter.3.cloned.1.call-update
  34.7 0.0 reduce-scatter.5.cloned.1.call-start
  34.7 31.5 %reduce-scatter.3.cloned.1.call-done = f32[8,64,2,2048]{3,1,2,0:T(8,128)} async-done(((f32[16,64,2,2048]{3,1,2,0:T(8,128)}), f32[8,64,2,2048]{3,1,2,0:T(8,128)}) %reduce-scatter.3.cloned.1.call-update) | async-done | bytes 8388624 | tf_op jit(solution)/shard_map/reduce_scatter | solution.py:33
  66.2 0.0 reduce-scatter.5.cloned.1.call-update
  66.2 172.6 %reduce-scatter.5.cloned.1.call-done = f32[1,64,2,2048]{3,1,2,0:T(8,128)} async-done(((f32[8,64,2,2048]{3,1,2,0:T(8,128)}), f32[1,64,2,2048]{3,1,2,0:T(8,128)}) %reduce-scatter.5.cloned.1.call-update) | async-done | bytes 1048592 | tf_op jit(solution)/shard_map/reduce_scatter | solution.py:34
  238.8 2.1 multiply_reduce_fusion
  240.9 9.1 %psum.35 = f32[]{:T(128)} all-reduce(f32[]{:T(128)} %multiply_reduce_fusion), channel_id=1, replica_groups=mesh['tp_0'=4,'tp_1'=2,'dp_0'=4,'dp_1'=2,'dp_2'=2] {'tp_0'}, use_global_device_ids=true, to_apply=%region_3.0 | all-reduce | flops 1 | bytes 8 | tf_op jit(solution)/shard_map/psum | solution.py:38
  250.0 5.9 %psum.36 = f32[]{:T(128)} all-reduce(f32[]{:T(128)} %psum.35), channel_id=1, replica_groups=mesh['tp_0'=4,'tp_1'=2,'dp_0'=4,'dp_1'=2,'dp_2'=2] {'tp_1'}, use_global_device_ids=true, to_apply=%region_4.0 | all-reduce | flops 1 | bytes 8 | tf_op jit(solution)/shard_map/psum | solution.py:38
  255.8 9.3 %psum.37 = f32[]{:T(128)} all-reduce(f32[]{:T(128)} %psum.36), channel_id=1, replica_groups=mesh['tp_0'=4,'tp_1'=2,'dp_0'=4,'dp_1'=2,'dp_2'=2] {'dp_0'}, use_global_device_ids=true, to_apply=%region_5.0 | all-reduce | flops 1 | bytes 8 | tf_op jit(solution)/shard_map/psum | solution.py:38
  265.1 4.4 %psum.38 = f32[]{:T(128)} all-reduce(f32[]{:T(128)} %psum.37), channel_id=1, replica_groups=mesh['tp_0'=4,'tp_1'=2,'dp_0'=4,'dp_1'=2,'dp_2'=2] {'dp_1'}, use_global_device_ids=true, to_apply=%region_6.0 | all-reduce | flops 1 | bytes 8 | tf_op jit(solution)/shard_map/psum | solution.py:38
  269.5 9.8 %psum.39 = f32[]{:T(128)} all-reduce(f32[]{:T(128)} %psum.38), channel_id=1, replica_groups=mesh['tp_0'=4,'tp_1'=2,'dp_0'=4,'dp_1'=2,'dp_2'=2] {'dp_2'}, use_global_device_ids=true, to_apply=%region_7.0 | all-reduce | flops 1 | bytes 8 | tf_op jit(solution)/shard_map/psum | solution.py:38
  280.1 4.5 %fusion.2 = (bf16[64,2,2048]{2,0,1:T(8,128)(2,1)S(1)}, f32[64,2,2048]{2,0,1:T(8,128)S(1)}, f32[64,2,2048]{2,0,1:T(8,128)S(1)}, f32[64,2,2048]{2,0,1:T(8,128)S(1)}) fusion(f32[64,2,2048]{2,1,0:T(2,128)} %param.7, f32[1,64,2,2048]{3,1,2,0:T(8,128)} %reduce-scatter.5.cloned.1.call-done, f32[]{:T(128)S(6)} %div.18, f32[64,2,2048]{2,1,0:T(2,128)} %param.8, ...), kind=kLoop, calls=%fused_computation.8 | loop fusion | flops 4456448 | bytes 7864324 | tf_op jit(solution)/shard_map/convert_element_type | solution.py:71
  284.6 0.5 copy.17
  285.1 7.6 %stack.2 = bf16[16,64,2,2048]{3,2,1,0:T(2,128)(2,1)} broadcast(bf16[64,2,2048]{2,1,0:T(2,128)(2,1)S(1)} %copy.17), dimensions={1,2,3} | broadcast | bytes 8912896 | tf_op jit(solution)/shard_map/stack | solution.py:73
  292.7 4.8 %all-to-all-start = ((bf16[16,64,2,2048]{3,2,1,0:T(2,128)(2,1)}), bf16[16,64,2,2048]{3,2,1,0:T(2,128)(2,1)}, u32[]{:S(2)}, u32[]{:S(2)}) async-start(bf16[16,64,2,2048]{3,2,1,0:T(2,128)(2,1)} %stack.2), calls=%async_computation.2 | async-start | bytes 16777216 | tf_op jit(solution)/shard_map/all_to_all | solution.py:73
  297.6 1.8 copy.18
  299.3 1.8 copy.19
  301.1 1.8 copy.20
  302.9 89.2 %all-to-all-done = bf16[16,64,2,2048]{3,2,1,0:T(2,128)(2,1)} async-done(((bf16[16,64,2,2048]{3,2,1,0:T(2,128)(2,1)}), bf16[16,64,2,2048]{3,2,1,0:T(2,128)(2,1)}, u32[]{:S(2)}, u32[]{:S(2)}) %all-to-all-start) | async-done | bytes 8388640 | tf_op jit(solution)/shard_map/all_to_all | solution.py:73
  392.1 8.0 %copy.33 = bf16[1024,2,2048]{2,1,0:T(2,128)(2,1)} copy(bf16[1024,2,2048]{2,1,0:T(2,128)(2,1)} %bitcast.5) | data formatting | bytes 16777216
Async XLA Ops:
  7.2 59.0 %reduce-scatter.3.cloned.1.call-start = ((), (), s32[]{:S(2)}) async-start(), calls=%async_computation.3 | async-start | bytes 25165824 | tf_op jit(solution)/shard_map/reduce_scatter | solution.py:33
  34.7 204.1 %reduce-scatter.5.cloned.1.call-start = ((), (), s32[]{:S(2)}) async-start(), calls=%async_computation.4 | async-start | bytes 9437184 | tf_op jit(solution)/shard_map/reduce_scatter | solution.py:34
  292.7 99.4 %all-to-all-start = ((bf16[16,64,2,2048]{3,2,1,0:T(2,128)(2,1)}), bf16[16,64,2,2048]{3,2,1,0:T(2,128)(2,1)}, u32[]{:S(2)}, u32[]{:S(2)}) async-start(bf16[16,64,2,2048]{3,2,1,0:T(2,128)(2,1)} %stack.2), calls=%async_computation.2 | async-start | bytes 16777216 | tf_op jit(solution)/shard_map/all_to_all | solution.py:73
Sparse Core Ops, SparseCore 0:
  34.8 31.3 reduce-scatter.2
  68.6 170.1 reduce-scatter.4
